TPU v7x, 256 devices: a whole 4x4x8 slice. The times are simulated.
256 devices in a mesh: pair: 16 (over y_hi, x, core), tile: 16 (over y_lo, z).
Axes of the slice: x: 4, y: 4 (y_hi: 2, y_lo: 2; y = y_hi * 2 + y_lo), z: 8, core: 2. Of those that a mesh axis runs over, the one named last changes fastest.
Arguments:
- fixed: float32 [32768, 2048], P('pair', 'tile'), parts along dimension 0, may hold values from -6 to 6
- moving: float32 [32768, 2048], P('pair', 'tile'), parts along dimension 0, may hold values from -6 to 6
- offsets: int32 [2, 32768, 2048], P(None, ('pair', 'tile')), parts along dimension 1, may hold values from -3 to 3
- fractions: float32 [2, 32768, 2048], P(None, ('pair', 'tile')), parts along dimension 1, may hold values from 0 to 1
Outputs:
- warped: float32 [32768, 2048], P(('pair', 'tile')), parts along dimension 0
There are 16 independent parts, one for each index of `pair`. A program takes and returns all parts, laid end to end along the dimension named above; each array names one. Nothing has to cross between parts.
All inputs are finite; a program needn't handle non-finite values.
Results may differ from a plain program's by a relative error of at most 0.00002.
Values sent between devices are 32-bit elements; how exact they have to be, the bound alone decides.
A program may use at most 64 MiB of HBM per device.

v0:
```python
import jax
import jax.numpy as jnp
from jax import lax
from jax.sharding import PartitionSpec as P

RADIUS = 4
REACH = 3


def extended_2(block, sides, width):
    for axis, dim in sides:
        count = lax.axis_size(axis)
        forward = [(i, i + 1) for i in range(count - 1)]
        backward = [(target, source) for source, target in forward]
        low = lax.ppermute(
            lax.slice_in_dim(block, block.shape[dim] - width, None, axis=dim), axis, forward
        )
        high = lax.ppermute(lax.slice_in_dim(block, 0, width, axis=dim), axis, backward)
        block = jnp.concatenate([low, block, high], axis=dim)
    return block


def window_sum(extended):
    row_total = extended.shape[0] - 2 * RADIUS
    column_total = extended.shape[1] - 2 * RADIUS
    rows_summed = extended[0:row_total, :]
    for shift in range(1, 2 * RADIUS + 1):
        rows_summed = rows_summed + extended[shift : shift + row_total, :]
    result = rows_summed[:, 0:column_total]
    for shift in range(1, 2 * RADIUS + 1):
        result = result + rows_summed[:, shift : shift + column_total]
    return result


def similarity(fixed_ext, moving_ext):
    window_count = float((2 * RADIUS + 1) ** 2)
    fixed_sum = window_sum(fixed_ext)
    moving_sum = window_sum(moving_ext)
    fixed_square = window_sum(fixed_ext * fixed_ext)
    moving_square = window_sum(moving_ext * moving_ext)
    cross_sum = window_sum(fixed_ext * moving_ext)
    fixed_var = fixed_square - fixed_sum * fixed_sum / window_count
    moving_var = moving_square - moving_sum * moving_sum / window_count
    covariance = cross_sum - fixed_sum * moving_sum / window_count
    correlation = covariance / jnp.sqrt(fixed_var * moving_var + 0.001)
    return 0.5 * (1.0 + correlation)


def sample_corners(padded, offsets, band_rows, column_total, margin):
    zeros = jnp.zeros((band_rows, column_total), jnp.float32)
    left_rows = []
    right_rows = []
    for row_shift in range(-REACH, REACH + 2):
        slab = padded[margin + row_shift : margin + row_shift + band_rows, :]
        left_pick = zeros
        right_pick = zeros
        for col_shift in range(-REACH, REACH + 1):
            chosen = offsets[1] == col_shift
            start = margin + col_shift
            left_pick = jnp.where(chosen, slab[:, start : start + column_total], left_pick)
            right_pick = jnp.where(
                chosen, slab[:, start + 1 : start + 1 + column_total], right_pick
            )
        left_rows.append(left_pick)
        right_rows.append(right_pick)
    top_left, top_right, bottom_left, bottom_right = (zeros, zeros, zeros, zeros)
    for row_shift in range(-REACH, REACH + 1):
        chosen = offsets[0] == row_shift
        place = row_shift + REACH
        top_left = jnp.where(chosen, left_rows[place], top_left)
        top_right = jnp.where(chosen, right_rows[place], top_right)
        bottom_left = jnp.where(chosen, left_rows[place + 1], bottom_left)
        bottom_right = jnp.where(chosen, right_rows[place + 1], bottom_right)
    return (top_left, top_right, bottom_left, bottom_right)


def on_device(fixed, moving, offsets, fractions):
    margin = REACH + 1
    band_rows = offsets.shape[1]
    column_total = offsets.shape[2]
    depth = max(RADIUS, margin)
    banded = lax.all_to_all(
        jnp.stack((fixed, moving)), "tile", split_axis=1, concat_axis=2, tiled=True
    )
    deepened = extended_2(banded, (("tile", 1),), depth)
    window_rows = deepened
    window_rows = jnp.pad(window_rows, ((0, 0), (0, 0), (RADIUS, RADIUS)))
    confidence = similarity(window_rows[0], window_rows[1])
    moving_rows = deepened[1, depth - margin : depth + band_rows + margin, :]
    padded = jnp.pad(moving_rows, ((0, 0), (margin, margin)))
    top_left, top_right, bottom_left, bottom_right = sample_corners(
        padded, offsets, band_rows, column_total, margin
    )
    row_weight = confidence * fractions[0]
    column_weight = confidence * fractions[1]
    upper = (1.0 - column_weight) * top_left + column_weight * top_right
    lower = (1.0 - column_weight) * bottom_left + column_weight * bottom_right
    return (1.0 - row_weight) * upper + row_weight * lower


def solution(mesh):
    placed = (
        P("pair", "tile"),
        P("pair", "tile"),
        P(None, ("pair", "tile"), None),
        P(None, ("pair", "tile"), None),
    )
    return jax.shard_map(
        on_device, mesh=mesh, in_specs=placed, out_specs=P(("pair", "tile"), None), check_vma=False
    )
```

profile of v0, /device:TPU:8, one launch (start us, length us, event | category | flops | bytes accessed | tf_op | source)
XLA Modules:
  0.0 123.0 jit_solution(3653359728250834409)
XLA Ops:
  0.0 3.1 %pad_maximum_fusion.1 = f32[2,2048,128]{2,0,1:T(2,128)S(1)} fusion(f32[1,2048,128]{2,0,1:T(1,128)} %bitcast.109, f32[1,2048,128]{2,0,1:T(1,128)} %bitcast.110), kind=kLoop, calls=%fused_computation.5 | loop fusion | flops 524288 | bytes 4194304 | tf_op jit(solution)/shard_map/stack | solution.py:83
  3.1 57.9 %all_to_all.18 = f32[2,2048,128]{2,0,1:T(2,128)S(1)} all-to-all(f32[2,2048,128]{2,0,1:T(2,128)S(1)} %pad_maximum_fusion.1), channel_id=1, replica_groups=mesh['pair'=16,'tile'=16] {'tile'}, dimensions={1} | all-to-all | bytes 4194304 | tf_op jit(solution)/shard_map/all_to_all | solution.py:82
  61.1 0.0 copy-start.2
  61.1 1.3 %copy-done.2 = f32[2,2048,128]{2,0,1:T(2,128)} copy-done((f32[2,2048,128]{2,0,1:T(2,128)}, f32[2,2048,128]{2,0,1:T(2,128)S(1)}, u32[]{:S(2)}) %copy-start.2) | copy-done | bytes 2097176
  62.4 2.6 %copy.6 = f32[2,128,16,128]{3,2,1,0:T(8,128)} copy(f32[2,128,16,128]{3,0,1,2:T(2,128)S(1)} %bitcast.106) | data formatting | bytes 4194304 | tf_op jit(solution)/shard_map/all_to_all | solution.py:82
  64.9 1.7 %all_to_all.16 = f32[2,128,2048]{2,1,0:T(8,128)S(1)} reshape(f32[2,128,16,128]{3,2,1,0:T(8,128)} %copy.6) | data formatting | bytes 4194304 | tf_op jit(solution)/shard_map/all_to_all | solution.py:82
  66.7 0.0 copy-start
  66.7 4.1 %collective-permute-start = (f32[2,4,2048]{2,1,0:T(4,128)S(1)}, f32[2,4,2048]{2,1,0:T(4,128)S(1)}, u32[]{:S(2)}, u32[]{:S(2)}) collective-permute-start(f32[2,4,2048]{2,1,0:T(4,128)S(1)} %get-tuple-element.10), channel_id=1, source_target_pairs={{0,1},{1,2},{2,3},{3,4},{4,5},{5,6},{6,7},{7,8},{8,9},{9,10},{10,1... | collective-permute-start | bytes 196616 | tf_op jit(solution)/shard_map/ppermute | solution.py:15
  70.8 0.0 copy-start.3
  70.8 4.2 %collective-permute-start.1 = (f32[2,4,2048]{2,1,0:T(4,128)S(1)}, f32[2,4,2048]{2,1,0:T(4,128)S(1)}, u32[]{:S(2)}, u32[]{:S(2)}) collective-permute-start(f32[2,4,2048]{2,1,0:T(4,128)S(1)} %get-tuple-element.11), channel_id=1, source_target_pairs={{1,0},{2,1},{3,2},{4,3},{5,4},{6,5},{7,6},{8,7},{9,8},{10,9},{11,1... | collective-permute-start | bytes 196616 | tf_op jit(solution)/shard_map/ppermute | solution.py:18
  75.0 1.5 %constant_dynamic-update-slice_fusion.1 = f32[2,132,2048]{2,1,0:T(8,128)} fusion(f32[2,128,2048]{2,1,0:T(8,128)S(1)} %all_to_all.16), kind=kLoop, calls=%fused_computation.139 | loop fusion | bytes 4194304
  76.5 0.0 copy-done.3
  76.5 1.1 slice.1100
  77.6 1.6 %copy.7 = f32[1,128,16,128]{3,2,1,0:T(8,128)} copy(f32[1,128,16,128]{3,0,1,2:T(1,128)S(1)} %slice.1100) | data formatting | bytes 2097152 | tf_op jit(solution)/shard_map/slice | solution.py:60
  79.1 0.0 collective-permute-done
  79.1 0.0 collective-permute-done.1
  79.1 0.0 copy-done
  79.2 0.3 pad_maximum_fusion
  79.4 0.0 copy-start.1
  79.4 0.1 slice_bitcast_fusion
  79.5 1.3 %copy-done.1 = f32[2,136,2048]{2,1,0:T(8,128)} copy-done((f32[2,136,2048]{2,1,0:T(8,128)}, f32[2,136,2048]{2,1,0:T(8,128)S(1)}, u32[]{:S(2)}) %copy-start.1) | copy-done | bytes 2228248
  80.8 6.3 %add_bitcast_fusion = (f32[128,2056]{1,0:T(8,128)S(1)}, f32[128,2056]{1,0:T(8,128)S(1)}) fusion(f32[2,136,2048]{2,1,0:T(8,128)S(1)} %pad_maximum_fusion), kind=kLoop, calls=%fused_computation.34 | loop fusion | flops 4210688 | bytes 4333568 | tf_op jit(solution)/shard_map/add | solution.py:28
  87.1 3.5 %fusion.33 = (f32[1,136,2056]{2,1,0:T(8,128)S(1)}, f32[1,136,2056]{2,1,0:T(8,128)S(1)}, f32[1,136,2056]{2,1,0:T(8,128)S(1)}) fusion(f32[2,136,2048]{2,1,0:T(8,128)} %copy-done.1), kind=kLoop, calls=%fused_computation.136 | loop fusion | flops 838848 | bytes 5583616 | tf_op jit(solution)/shard_map/mul | solution.py:41
  90.6 0.8 fusion.2
  91.4 1.6 %fusion = (f32[128,2056]{1,0:T(8,128)S(1)}, f32[128,2056]{1,0:T(8,128)S(1)}) fusion(f32[1,136,2056]{2,1,0:T(8,128)S(1)} %get-tuple-element.9, f32[1,136,2056]{2,1,0:T(8,128)S(1)} %get-tuple-element.8), kind=kLoop, calls=%fused_computation.8 | loop fusion | flops 4210688 | bytes 21053440 | tf_op jit(solution)/shard_map/add | solution.py:28
  93.1 0.7 constant_dynamic-update-slice_fusion
  93.7 29.3 %multiply_add_fusion = f32[128,2048]{1,0:T(8,128)} fusion(f32[2,132,2048]{2,1,0:T(8,128)} %constant_dynamic-update-slice_fusion, f32[16,8,16,128]{3,2,1,0:T(8,128)} %bitcast.108, f32[2,128,2048]{2,1,0:T(8,128)} %copy-done, f32[2,4,2048]{2,1,0:T(4,128)S(1)} %collective-permute-done, f32[136,2048]{1,0:T(8,128)S(1)} %slice_bitcast_fusion, ...), kind=kLoop, calls=%fused_computation.131 | loop fusion | flops 58720256 | bytes 60948480 | tf_op jit(solution)/shard_map/add | solution.py:98
  (1 shorter events, 0.0 us)
Async XLA Ops:
  61.1 1.3 %copy-start.2 = (f32[2,2048,128]{2,0,1:T(2,128)}, f32[2,2048,128]{2,0,1:T(2,128)S(1)}, u32[]{:S(2)}) copy-start(f32[2,2048,128]{2,0,1:T(2,128)S(1)} %all_to_all.18) | copy-start | bytes 6291460
  66.7 12.5 %copy-start = (f32[2,128,2048]{2,1,0:T(8,128)}, f32[2,128,2048]{2,1,0:T(8,128)S(1)}, u32[]{:S(2)}) copy-start(f32[2,128,2048]{2,1,0:T(8,128)S(1)} %all_to_all.16) | copy-start | bytes 6291460
  66.7 12.4 %collective-permute-start = (f32[2,4,2048]{2,1,0:T(4,128)S(1)}, f32[2,4,2048]{2,1,0:T(4,128)S(1)}, u32[]{:S(2)}, u32[]{:S(2)}) collective-permute-start(f32[2,4,2048]{2,1,0:T(4,128)S(1)} %get-tuple-element.10), channel_id=1, source_target_pairs={{0,1},{1,2},{2,3},{3,4},{4,5},{5,6},{6,7},{7,8},{8,9},{9,10},{10,1... | collective-permute-start | bytes 196616 | tf_op jit(solution)/shard_map/ppermute | solution.py:15
  70.8 5.7 %copy-start.3 = (f32[2,2048,128]{2,0,1:T(2,128)S(1)}, f32[2,2048,128]{2,0,1:T(2,128)}, u32[]{:S(2)}) copy-start(f32[2,2048,128]{2,0,1:T(2,128)} %copy-done.2) | copy-start | bytes 6291460
  70.8 8.4 %collective-permute-start.1 = (f32[2,4,2048]{2,1,0:T(4,128)S(1)}, f32[2,4,2048]{2,1,0:T(4,128)S(1)}, u32[]{:S(2)}, u32[]{:S(2)}) collective-permute-start(f32[2,4,2048]{2,1,0:T(4,128)S(1)} %get-tuple-element.11), channel_id=1, source_target_pairs={{1,0},{2,1},{3,2},{4,3},{5,4},{6,5},{7,6},{8,7},{9,8},{10,9},{11,1... | collective-permute-start | bytes 196616 | tf_op jit(solution)/shard_map/ppermute | solution.py:18
  79.4 1.3 %copy-start.1 = (f32[2,136,2048]{2,1,0:T(8,128)}, f32[2,136,2048]{2,1,0:T(8,128)S(1)}, u32[]{:S(2)}) copy-start(f32[2,136,2048]{2,1,0:T(8,128)S(1)} %pad_maximum_fusion) | copy-start | bytes 6684676
where the time goes:
time: 123 us
  blocking collectives  57.9 us (47%)
  other arithmetic  45 us (37%)
  local copies, waits for them, and re-layouts  11.7 us (10%)
  starting transfers between devices  8.26 us (7%)
    all_to_all x1, blocking collectives, on_device(): lax.all_to_all(jnp.stack((fixed, moving)), 'tile', split_axis=1, concat_a...  57.9 us
    add x1, other arithmetic, on_device(): return (1.0 - row_weight) * upper + row_weight * lower  29.3 us
    add x3, other arithmetic, window_sum(): rows_summed = rows_summed + extended[shift:shift + row_total, :]  8.73 us
    all_to_all x2, local copies, waits for them, and re-layouts, on_device(): lax.all_to_all(jnp.stack((fixed, moving)), 'tile', split_axis=1, concat_a...  4.27 us
    ppermute x1, starting transfers between devices, extended_2(): lax.ppermute(lax.slice_in_dim(block, 0, width, axis=dim), axis, backward)  4.2 us
    ppermute x1, starting transfers between devices, extended_2(): lax.ppermute(lax.slice_in_dim(block, block.shape[dim] - width, None, axis...  4.06 us
    unnamed x9, local copies, waits for them, and re-layouts  4.06 us
    mul x1, other arithmetic, similarity(): cross_sum = window_sum(fixed_ext * moving_ext)  3.54 us
  transfers between devices with their start and end apart: 2, of which 0 were waited for; matrix products, arithmetic and copies ran while one was open for 3% of the time, Pallas kernels for 0%

commit v1 on v0

--- a/solution.py
+++ b/solution.py
@@ -79,8 +79,14 @@
     band_rows = offsets.shape[1]
     column_total = offsets.shape[2]
     depth = max(RADIUS, margin)
-    banded = lax.all_to_all(
-        jnp.stack((fixed, moving)), "tile", split_axis=1, concat_axis=2, tiled=True
+    banded = jnp.concatenate(
+        lax.all_to_all(
+            jnp.stack(jnp.split(jnp.stack((fixed, moving)), lax.axis_size("tile"), axis=1)),
+            "tile",
+            0,
+            0,
+        ),
+        axis=2,
     )
     deepened = extended_2(banded, (("tile", 1),), depth)
     window_rows = deepened

time: 123 us -> 112 us (0.911)
  local copies, waits for them, and re-layouts: 11.7 us -> 4.83 us
  other arithmetic: 45 us -> 40.9 us
    all_to_all x2 -> x0, local copies, waits for them, and re-layouts: 4.27 us -> none  [on_device(): lax.all_to_all(jnp.stack((fixed, moving)), 'tile', split_axis=1, concat_a...]
    another operation x1, other arithmetic: 3.13 us -> 0.01 us  [on_device(): jnp.stack(jnp.split(jnp.stack((fixed, moving)), lax.axis_size('tile'), ax...]
    mul x1, other arithmetic: 3.54 us -> 1.28 us  [similarity(): cross_sum = window_sum(fixed_ext * moving_ext)]
    unnamed x9 -> x7, local copies, waits for them, and re-layouts: 4.06 us -> 2.16 us
where the time goes in v1:
time: 112 us
  blocking collectives  57.9 us (52%)
  other arithmetic  40.9 us (37%)
  starting transfers between devices  7.95 us (7%)
  local copies, waits for them, and re-layouts  4.83 us (4%)
    all_to_all x1, blocking collectives, on_device(): lax.all_to_all(jnp.stack(jnp.split(jnp.stack((fixed, moving)), lax.axis_s...  57.9 us
    add x1, other arithmetic, on_device(): return (1.0 - row_weight) * upper + row_weight * lower  29.4 us
    add x3, other arithmetic, window_sum(): rows_summed = rows_summed + extended[shift:shift + row_total, :]  8.75 us
    ppermute x1, starting transfers between devices, extended_2(): lax.ppermute(lax.slice_in_dim(block, block.shape[dim] - width, None, axis...  4.06 us
    ppermute x1, starting transfers between devices, extended_2(): lax.ppermute(lax.slice_in_dim(block, 0, width, axis=dim), axis, backward)  3.89 us
  transfers between devices with their start and end apart: 2, of which 0 were waited for; matrix products, arithmetic and copies ran while one was open for 3% of the time, Pallas kernels for 0%

profile of v1, /device:TPU:8, one launch (start us, length us, event | category | flops | bytes accessed | tf_op | source)
XLA Modules:
  0.0 111.8 jit_solution(7493264195206224060)
XLA Ops:
  0.0 0.0 copy-start
  0.0 0.0 copy-start.1
  0.0 1.0 bitcast_dynamic-update-slice_fusion.14
  1.0 0.2 copy-done
  1.3 0.3 copy-done.1
  1.9 57.9 %all_to_all.5 = f32[16,2,128,128]{3,2,1,0:T(8,128)S(1)} all-to-all(f32[16,2,128,128]{3,2,1,0:T(8,128)S(1)} %fusion.51), channel_id=1, replica_groups=mesh['pair'=16,'tile'=16] {'tile'}, dimensions={0} | all-to-all | bytes 4194304 | tf_op jit(solution)/shard_map/all_to_all | solution.py:83
  59.8 0.2 copy_bitcast_fusion
  60.1 0.0 copy-start.2
  60.1 4.1 %collective-permute-start = (f32[2,4,2048]{2,1,0:T(4,128)S(1)}, f32[2,4,2048]{2,1,0:T(4,128)S(1)}, u32[]{:S(2)}, u32[]{:S(2)}) collective-permute-start(f32[2,4,2048]{2,1,0:T(4,128)S(1)} %get-tuple-element.10), channel_id=1, source_target_pairs={{0,1},{1,2},{2,3},{3,4},{4,5},{5,6},{6,7},{7,8},{8,9},{9,10},{10,1... | collective-permute-start | bytes 196616 | tf_op jit(solution)/shard_map/ppermute | solution.py:15
  64.2 3.9 %collective-permute-start.1 = (f32[2,4,2048]{2,1,0:T(4,128)S(1)}, f32[2,4,2048]{2,1,0:T(4,128)S(1)}, u32[]{:S(2)}, u32[]{:S(2)}) collective-permute-start(f32[2,4,2048]{2,1,0:T(4,128)S(1)} %get-tuple-element.11), channel_id=1, source_target_pairs={{1,0},{2,1},{3,2},{4,3},{5,4},{6,5},{7,6},{8,7},{9,8},{10,9},{11,1... | collective-permute-start | bytes 196616 | tf_op jit(solution)/shard_map/ppermute | solution.py:18
  68.1 1.6 %constant_dynamic-update-slice_fusion.1 = f32[2,132,2048]{2,1,0:T(8,128)} fusion(f32[16,2,128,128]{3,2,1,0:T(8,128)S(1)} %all_to_all.5), kind=kLoop, calls=%fused_computation.202 | loop fusion | bytes 4194304
  69.7 0.1 slice.1100
  69.7 1.6 %copy.6 = f32[1,128,16,128]{3,2,1,0:T(8,128)} copy(f32[1,128,16,128]{3,1,0,2:T(8,128)S(1)} %slice.1100) | data formatting | bytes 2097152 | tf_op jit(solution)/shard_map/slice | solution.py:60
  71.3 0.0 collective-permute-done
  71.3 0.0 collective-permute-done.1
  71.3 0.0 copy-done.2
  71.3 0.3 pad_maximum_fusion
  71.6 0.1 slice_bitcast_fusion
  71.7 6.3 %add_bitcast_fusion = (f32[128,2056]{1,0:T(8,128)S(1)}, f32[128,2056]{1,0:T(8,128)S(1)}) fusion(f32[2,136,2048]{2,1,0:T(8,128)S(1)} %pad_maximum_fusion), kind=kLoop, calls=%fused_computation.64 | loop fusion | flops 4210688 | bytes 4333568 | tf_op jit(solution)/shard_map/add | solution.py:28
  78.0 1.3 %fusion.33 = (f32[1,136,2056]{2,1,0:T(8,128)S(1)}, f32[1,136,2056]{2,1,0:T(8,128)S(1)}, f32[1,136,2056]{2,1,0:T(8,128)S(1)}) fusion(f32[2,136,2048]{2,1,0:T(8,128)S(1)} %pad_maximum_fusion), kind=kLoop, calls=%fused_computation.166 | loop fusion | flops 838848 | bytes 5583616 | tf_op jit(solution)/shard_map/mul | solution.py:41
  79.3 0.8 fusion.2
  80.1 1.6 %fusion = (f32[128,2056]{1,0:T(8,128)S(1)}, f32[128,2056]{1,0:T(8,128)S(1)}) fusion(f32[1,136,2056]{2,1,0:T(8,128)S(1)} %get-tuple-element.9, f32[1,136,2056]{2,1,0:T(8,128)S(1)} %get-tuple-element.8), kind=kLoop, calls=%fused_computation.38 | loop fusion | flops 4210688 | bytes 21053440 | tf_op jit(solution)/shard_map/add | solution.py:28
  81.8 0.6 constant_dynamic-update-slice_fusion
  82.4 29.4 %multiply_add_fusion = f32[128,2048]{1,0:T(8,128)} fusion(f32[2,132,2048]{2,1,0:T(8,128)} %constant_dynamic-update-slice_fusion, f32[16,8,16,128]{3,2,1,0:T(8,128)} %bitcast.178, f32[2,128,2048]{2,1,0:T(8,128)} %copy-done.2, f32[2,4,2048]{2,1,0:T(4,128)S(1)} %collective-permute-done, f32[136,2048]{1,0:T(8,128)S(1)} %slice_bitcast_fusion, ...), kind=kLoop, calls=%fused_computation.161 | loop fusion | flops 58720256 | bytes 60948480 | tf_op jit(solution)/shard_map/add | solution.py:104
  (16 shorter events, 0.2 us)
Async XLA Ops:
  0.0 1.3 %copy-start = (f32[2048,128]{1,0:T(8,128)S(1)}, f32[2048,128]{1,0:T(8,128)}, u32[]{:S(2)}) copy-start(f32[2048,128]{1,0:T(8,128)} %param.5) | copy-start | bytes 3145732
  0.0 1.6 %copy-start.1 = (f32[2048,128]{1,0:T(8,128)S(1)}, f32[2048,128]{1,0:T(8,128)}, u32[]{:S(2)}) copy-start(f32[2048,128]{1,0:T(8,128)} %param.4) | copy-start | bytes 3145732
  60.1 11.3 %copy-start.2 = (f32[2,128,2048]{2,1,0:T(8,128)}, f32[2,128,2048]{2,1,0:T(8,128)S(1)}, u32[]{:S(2)}) copy-start(f32[2,128,2048]{2,1,0:T(8,128)S(1)} %copy_bitcast_fusion) | copy-start | bytes 6291460
  60.1 11.2 %collective-permute-start = (f32[2,4,2048]{2,1,0:T(4,128)S(1)}, f32[2,4,2048]{2,1,0:T(4,128)S(1)}, u32[]{:S(2)}, u32[]{:S(2)}) collective-permute-start(f32[2,4,2048]{2,1,0:T(4,128)S(1)} %get-tuple-element.10), channel_id=1, source_target_pairs={{0,1},{1,2},{2,3},{3,4},{4,5},{5,6},{6,7},{7,8},{8,9},{9,10},{10,1... | collective-permute-start | bytes 196616 | tf_op jit(solution)/shard_map/ppermute | solution.py:15
  64.2 7.2 %collective-permute-start.1 = (f32[2,4,2048]{2,1,0:T(4,128)S(1)}, f32[2,4,2048]{2,1,0:T(4,128)S(1)}, u32[]{:S(2)}, u32[]{:S(2)}) collective-permute-start(f32[2,4,2048]{2,1,0:T(4,128)S(1)} %get-tuple-element.11), channel_id=1, source_target_pairs={{1,0},{2,1},{3,2},{4,3},{5,4},{6,5},{7,6},{8,7},{9,8},{10,9},{11,1... | collective-permute-start | bytes 196616 | tf_op jit(solution)/shard_map/ppermute | solution.py:18
